TPU v7x, 128 devices: a whole 4x4x4 slice. The times are simulated.
128 devices in a mesh: grp: 8 (over z, y_lo), dev: 16 (over x, y_hi, core).
Axes of the slice: x: 4, y: 4 (y_hi: 2, y_lo: 2; y = y_hi * 2 + y_lo), z: 4, core: 2. Of those that a mesh axis runs over, the one named last changes fastest.
Arguments:
- vertex_values: bfloat16 [8192, 128, 256], P(('grp', 'dev')), may hold values from -6 to 6
- position_domain_label: int32 [8192], P(('grp', 'dev')), may hold values from 0 to 64, as said below
- position_vertex_tally: int32 [8192], P(('grp', 'dev')), may hold values from 0 to 128, as said below
- normalizer_gain: float32 [256], replicated, may hold values from 0.1 to 1.9
- embedding_matrix: bfloat16 [256, 256], replicated, may hold values from -0.375 to 0.375
- partition_input_matrix: bfloat16 [256, 256], replicated, may hold values from -0.375 to 0.375
- partition_score_matrix: bfloat16 [32, 64], replicated, may hold values from -60 to 60
- softmax_sharpness: float32 [8], replicated, may hold values from 0.3 to 1
- partition_attention_maps: float32 [3, 32, 32], replicated, may hold values from -10 to 10
- readout_matrix: bfloat16 [256, 256], replicated, may hold values from -1.5 to 1.5
Outputs:
- updated: bfloat16 [8192, 128, 256], P(('grp', 'dev'))
Inputs may be any that keep to these rules, and one draw needn't show every extreme that they name: `position_domain_label`: on each device the used slots come first; a device may use none. Reading the devices in order and their used slots in order lists every mesh's blocks as one run, meshes in increasing order, each mesh 2 or more blocks. Exactly 4096 slots are used in all, and some device uses all 64 of its slots. `position_vertex_tally`: 128 in every used slot except the last block of each mesh, which holds 1 to 128; 0 in unused slots.
All inputs are finite; a program needn't handle non-finite values.
Results may differ from a plain program's by a relative error of at most 0.012.
The roundings to bfloat16 on the way count: a program that leaves them out, or rounds other values in their place, can miss the bound.
Values may be sent and summed in bfloat16 or wider, within the bound.
No kernel may reach another device: no remote copies, remote signals or barrier semaphores. Data moves between devices by JAX's collectives and lax.ppermute only.
A program may use at most 128 MiB of HBM per device.

v0:
```python
import jax
import jax.numpy as jnp
from jax import lax
from jax.sharding import PartitionSpec as P

MESHES = 64


def partition_routine(
    tile_sequence,
    vertex_tallies,
    domain_sequence,
    normalizer_gain,
    embedding_matrix,
    partition_input_matrix,
    partition_score_matrix,
    softmax_sharpness,
):
    tile_amount, tile_height, model_width = tile_sequence.shape
    attention_group_amount = softmax_sharpness.shape[0]
    head_width = model_width // attention_group_amount
    partition_amount = partition_score_matrix.shape[1]
    flattened = tile_sequence.reshape(tile_amount * tile_height, model_width).astype(jnp.float32)
    centre = flattened - jnp.mean(flattened, axis=1, keepdims=True)
    spread = jnp.mean(centre * centre, axis=1, keepdims=True)
    normed = (centre * lax.rsqrt(spread + 1e-05) * normalizer_gain).astype(jnp.bfloat16)
    features = jnp.dot(normed, embedding_matrix, preferred_element_type=jnp.float32).astype(
        jnp.bfloat16
    )
    middles = jnp.dot(normed, partition_input_matrix, preferred_element_type=jnp.float32).astype(
        jnp.bfloat16
    )
    partition_scores = jnp.dot(
        middles.reshape(-1, head_width), partition_score_matrix, preferred_element_type=jnp.float32
    )
    partition_scores = (
        partition_scores.reshape(tile_amount, tile_height, attention_group_amount, partition_amount)
        / softmax_sharpness[:, None]
    )
    living = (
        lax.broadcasted_iota(jnp.int32, (tile_amount, tile_height), 1) < vertex_tallies[:, None]
    ).astype(jnp.float32)
    partition_shares = (
        jax.nn.softmax(partition_scores, axis=-1) * living[:, :, None, None]
    ).astype(jnp.bfloat16)
    partial_sums = jnp.einsum(
        "bphm,bphd->bhmd",
        partition_shares,
        features.reshape(tile_amount, tile_height, attention_group_amount, head_width),
        preferred_element_type=jnp.float32,
    )
    partial_totals = jnp.sum(partition_shares.astype(jnp.float32), axis=1)
    one_hot = (
        domain_sequence[:, None] == lax.broadcasted_iota(jnp.int32, (tile_amount, MESHES), 1)
    ).astype(jnp.float32)
    domain_accumulated = jnp.dot(one_hot.T, partial_sums.reshape(tile_amount, -1))
    domain_share_accumulated = jnp.dot(one_hot.T, partial_totals.reshape(tile_amount, -1))
    return (
        partition_shares.reshape(
            tile_amount, tile_height, attention_group_amount * partition_amount
        ),
        domain_accumulated,
        domain_share_accumulated,
    )


def attend_tokens(domain_accumulated, domain_share_accumulated, partition_attention_maps):
    row_count, partition_amount = domain_share_accumulated.shape
    head_width = partition_attention_maps.shape[1]
    tokens = domain_accumulated.reshape(row_count, partition_amount, head_width) / (
        domain_share_accumulated[:, :, None] + 1.0
    )
    queries = jnp.einsum("rmd,de->rme", tokens, partition_attention_maps[0])
    key_rows = jnp.einsum("rmd,de->rme", tokens, partition_attention_maps[1])
    values = jnp.einsum("rmd,de->rme", tokens, partition_attention_maps[2])
    scores = jnp.einsum("rme,rne->rmn", queries, key_rows) * head_width ** (-0.5)
    token_probs = jax.nn.softmax(scores, axis=-1)
    blended = jnp.einsum("rmn,rne->rme", token_probs, values)
    return blended.reshape(row_count, partition_amount * head_width).astype(jnp.bfloat16)


def spread_phase(
    tile_sequence, vertex_tallies, domain_sequence, partition_shares, tokens, readout_matrix
):
    tile_amount, tile_height, model_width = tile_sequence.shape
    attention_group_amount = tokens.shape[0] // MESHES
    partition_amount = partition_shares.shape[2] // attention_group_amount
    head_width = model_width // attention_group_amount
    tables = tokens.reshape(MESHES, attention_group_amount, partition_amount, head_width)
    chosen = jnp.take(tables, jnp.minimum(domain_sequence, MESHES - 1), axis=0)
    blended = jnp.einsum(
        "bphm,bhmd->bphd",
        partition_shares.reshape(
            tile_amount, tile_height, attention_group_amount, partition_amount
        ),
        chosen,
        preferred_element_type=jnp.float32,
    ).astype(jnp.bfloat16)
    projected = jnp.dot(
        blended.reshape(-1, model_width), readout_matrix, preferred_element_type=jnp.float32
    )
    living = (
        lax.broadcasted_iota(jnp.int32, (tile_amount, tile_height), 1) < vertex_tallies[:, None]
    ).astype(jnp.float32)
    result = (
        tile_sequence.reshape(-1, model_width).astype(jnp.float32) + projected
    ) * living.reshape(-1, 1)
    return result.reshape(tile_amount, tile_height, model_width).astype(jnp.bfloat16)


def on_device(
    vertex_values,
    position_domain_label,
    position_vertex_tally,
    normalizer_gain,
    embedding_matrix,
    partition_input_matrix,
    partition_score_matrix,
    softmax_sharpness,
    partition_attention_maps,
    readout_matrix,
):
    slot_total, tile_height, model_width = vertex_values.shape
    attention_group_amount = softmax_sharpness.shape[0]
    partition_amount = partition_score_matrix.shape[1]
    group_count = slot_total // 16
    grouped = (
        vertex_values.reshape(group_count, 16, tile_height, model_width),
        position_vertex_tally.reshape(group_count, 16),
        position_domain_label.reshape(group_count, 16),
    )

    def gather_step(running, lookup_element):
        partition_shares, domain_accumulated, domain_share_accumulated = partition_routine(
            lookup_element[0],
            lookup_element[1],
            lookup_element[2],
            normalizer_gain,
            embedding_matrix,
            partition_input_matrix,
            partition_score_matrix,
            softmax_sharpness,
        )
        return (
            (running[0] + domain_accumulated, running[1] + domain_share_accumulated),
            partition_shares,
        )

    initial = (
        jnp.zeros((MESHES, model_width * partition_amount), jnp.float32),
        jnp.zeros((MESHES, attention_group_amount * partition_amount), jnp.float32),
    )
    (domain_accumulated, domain_share_accumulated), partition_shares = lax.scan(
        gather_step, initial, grouped
    )
    whole_sums, whole_totals = lax.psum(
        (
            domain_accumulated.reshape(MESHES * attention_group_amount, -1),
            domain_share_accumulated.reshape(MESHES * attention_group_amount, -1),
        ),
        ("grp", "dev"),
    )
    tokens = attend_tokens(whole_sums, whole_totals, partition_attention_maps)

    def spread_step(lookup_element):
        return spread_phase(
            lookup_element[0],
            lookup_element[1],
            lookup_element[2],
            lookup_element[3],
            tokens,
            readout_matrix,
        )

    return lax.map(spread_step, grouped + (partition_shares,)).reshape(vertex_values.shape)


def solution(mesh):
    return jax.shard_map(
        on_device,
        mesh=mesh,
        in_specs=(
            P(("grp", "dev"), None, None),
            P(("grp", "dev")),
            P(("grp", "dev")),
            P(),
            P(),
            P(),
            P(),
            P(),
            P(),
            P(),
        ),
        out_specs=P(("grp", "dev"), None, None),
        check_vma=False,
    )
```

profile of v0, /device:TPU:1, one launch (start us, length us, event | category | flops | bytes accessed | tf_op | source)
XLA Modules:
  0.0 490.3 jit_solution(10821527517631763876)
XLA Ops:
  8.0 115.3 %while.26 = (s32[]{:T(128)}, f32[64,16384]{1,0:T(8,128)}, f32[64,512]{1,0:T(8,128)S(1)}, bf16[4,16,128,512]{2,3,1,0:T(8,128)(2,1)}, s32[4,16]{1,0:T(4,128)S(1)},...) while((s32[]{:T(128)}, f32[64,16384]{1,0:T(8,128)}, ...), condition=%wide.region_6.7_spmd.clone, body=%wide.region_0.6_spmd.clone.sunk | while | flops 723058752 | bytes 48028012 | solution.py:153
  14.7 3.6 fusion.111
  18.4 3.4 convert_reduce_fusion.5
  24.9 2.1 fusion.112
  27.0 3.5 reshape.222
  30.5 2.8 convolution_add_fusion.5
  41.9 3.6 fusion.111
  45.6 3.4 convert_reduce_fusion.5
  52.1 2.1 fusion.112
  54.2 3.5 reshape.222
  57.7 5.0 %convolution_add_fusion.5 = f32[64,16384]{1,0:T(8,128)} fusion(bf16[16,16384]{1,0:T(8,128)(2,1)S(1)} %reshape.222, f32[64,16384]{1,0:T(8,128)} %get-tuple-element.383, pred[]{:T(512)S(6)} %compare.3, s32[16]{0:T(128)S(1)} %get-tuple-element.366), kind=kOutput, calls=%fused_computation.27.clone.1 | convolution fusion | flops 35652608 | bytes 8912961 | tf_op jit(solution)/shard_map/while/body/eval_jaxpr/dot_general | solution.py:56
  71.3 3.6 fusion.111
  74.9 3.4 convert_reduce_fusion.5
  83.5 3.5 reshape.222
  87.0 5.0 %convolution_add_fusion.5 = f32[64,16384]{1,0:T(8,128)} fusion(bf16[16,16384]{1,0:T(8,128)(2,1)S(1)} %reshape.222, f32[64,16384]{1,0:T(8,128)} %get-tuple-element.383, pred[]{:T(512)S(6)} %compare.3, s32[16]{0:T(128)S(1)} %get-tuple-element.366), kind=kOutput, calls=%fused_computation.27.clone.1 | convolution fusion | flops 35652608 | bytes 8912961 | tf_op jit(solution)/shard_map/while/body/eval_jaxpr/dot_general | solution.py:56
  100.6 3.6 fusion.111
  104.3 3.4 convert_reduce_fusion.5
  112.9 3.5 reshape.222
  116.4 5.0 %convolution_add_fusion.5 = f32[64,16384]{1,0:T(8,128)} fusion(bf16[16,16384]{1,0:T(8,128)(2,1)S(1)} %reshape.222, f32[64,16384]{1,0:T(8,128)} %get-tuple-element.383, pred[]{:T(512)S(6)} %compare.3, s32[16]{0:T(128)S(1)} %get-tuple-element.366), kind=kOutput, calls=%fused_computation.27.clone.1 | convolution fusion | flops 35652608 | bytes 8912961 | tf_op jit(solution)/shard_map/while/body/eval_jaxpr/dot_general | solution.py:56
  123.3 5.0 %reshape.192 = f32[512,2048]{1,0:T(8,128)} reshape(f32[64,16384]{1,0:T(8,128)} %get-tuple-element.111) | data formatting | bytes 8388608 | tf_op jit(solution)/shard_map/reshape | solution.py:158
  129.2 157.6 %all-reduce.3.cloned.1.call-done = (f32[512,2048]{1,0:T(8,128)}, f32[512,64]{0,1:T(8,128)}) async-done(((f32[512,2048]{1,0:T(8,128)}, f32[512,64]{0,1:T(8,128)}), (f32[512,2048]{1,0:T(8,128)}, f32[512,64]{0,1:T(8,128)})) %all-reduce.3.cloned.1.call-update) | async-done | bytes 4325392 | tf_op jit(solution)/shard_map/psum | solution.py:156
  287.8 2.5 div.47
  290.3 5.4 %copy.52 = f32[512,2048]{1,0:T(8,128)} copy(f32[512,2048]{0,1:T(8,128)} %bitcast.167) | data formatting | bytes 8388608 | tf_op jit(solution)/shard_map/div | solution.py:70
  295.7 5.7 %div.49 = bf16[512,2048]{1,0:T(8,128)(2,1)} divide(f32[512,2048]{1,0:T(8,128)} %get-tuple-element.218, f32[512,2048]{1,0:T(8,128)} %copy.52) | non-fusion elementwise | flops 1048576 | bytes 10485760 | tf_op jit(solution)/shard_map/div | solution.py:70
  301.3 3.0 copy.53
  304.4 2.1 fusion.39
  308.5 2.1 fusion.35
  310.6 8.8 %copy.56 = bf16[512,64,32]{1,2,0:T(8,128)(2,1)} copy(bf16[512,64,32]{0,2,1:T(8,128)(2,1)} %fusion.39) | data formatting | bytes 4194304 | tf_op jit(solution)/shard_map/rmd,de->rme/dot_general | solution.py:73
  319.3 8.9 %copy.57 = bf16[512,64,32]{1,2,0:T(8,128)(2,1)} copy(bf16[512,64,32]{0,2,1:T(8,128)(2,1)} %fusion.37) | data formatting | bytes 4194304 | tf_op jit(solution)/shard_map/rmd,de->rme/dot_general | solution.py:74
  328.3 7.9 %copy.60 = bf16[512,64,32]{1,2,0:T(8,128)(2,1)} copy(bf16[512,64,32]{0,2,1:T(8,128)(2,1)S(1)} %copy-done) | data formatting | bytes 4194304 | tf_op jit(solution)/shard_map/rmd,de->rme/dot_general | solution.py:75
  336.1 12.5 %multiply_reduce_fusion.1 = (f32[512,64]{1,0:T(8,128)S(1)}, f32[512,64,64]{1,2,0:T(8,128)}) fusion(bf16[512,64,32]{1,2,0:T(8,128)(2,1)} %copy.56, bf16[512,64,32]{1,2,0:T(8,128)(2,1)} %copy.57), kind=kOutput, calls=%fused_computation.61 | convolution fusion | flops 138379264 | bytes 12713984 | tf_op jit(solution)/shard_map/rme,rne->rmn/dot_general | solution.py:76
  348.7 10.3 %fusion.28 = f32[512,64]{1,0:T(8,128)S(1)} fusion(f32[512,64,64]{1,2,0:T(8,128)} %get-tuple-element.229, f32[512,64]{1,0:T(8,128)S(1)} %get-tuple-element.228), kind=kLoop, calls=%fused_computation.62 | loop fusion | flops 6258688 | bytes 8650752 | tf_op jit(solution)/shard_map/reduce_sum | solution.py:77
  359.0 10.4 %fusion.32 = bf16[512,64,32]{1,2,0:T(8,128)(2,1)} fusion(bf16[512,64,32]{1,2,0:T(8,128)(2,1)} %copy.60, f32[512,64,64]{1,2,0:T(8,128)} %get-tuple-element.229, f32[512,64]{1,0:T(8,128)S(1)} %fusion.28, f32[512,64]{1,0:T(8,128)S(1)} %get-tuple-element.228), kind=kOutput, calls=%fused_computation.66 | convolution fusion | flops 140509184 | bytes 12845056 | tf_op jit(solution)/shard_map/rmn,rne->rme/dot_general | solution.py:78
  369.4 6.9 %copy.61 = bf16[512,64,32]{0,2,1:T(8,128)(2,1)} copy(bf16[512,64,32]{1,2,0:T(8,128)(2,1)} %fusion.32) | data formatting | bytes 4194304 | tf_op jit(solution)/shard_map/convert_element_type | solution.py:79
  376.3 2.9 copy.62
  379.3 104.2 %while.25 = (s32[]{:T(128)}, bf16[4,16,128,256]{3,2,1,0:T(8,128)(2,1)}, bf16[4,16,128,256]{3,2,1,0:T(8,128)(2,1)}, s32[4,16]{1,0:T(4,128)S(1)}, bf16[512,2048]{1...) while((s32[]{:T(128)}, ...), condition=%wide.region_12.13_spmd, body=%wide.region_11.12_spmd.sunk | while | flops 338433216 | bytes 26891408 | solution.py:175
  379.6 8.0 %reshape.221 = bf16[64,8,64,32]{3,2,1,0:T(8,128)(2,1)} reshape(bf16[512,2048]{1,0:T(8,128)(2,1)S(1)} %get-tuple-element.432) | data formatting | bytes 4194304 | tf_op jit(solution)/shard_map/while/body/eval_jaxpr/reshape | solution.py:89
  387.6 8.6 %copy.92 = bf16[64,8,64,32]{2,3,1,0:T(8,128)(2,1)} copy(bf16[64,8,64,32]{3,2,1,0:T(8,128)(2,1)} %reshape.221) | data formatting | bytes 4194304 | tf_op jit(solution)/shard_map/while/body/eval_jaxpr/reshape | solution.py:89
  396.2 2.9 gather_fusion
  405.6 8.0 %reshape.221 = bf16[64,8,64,32]{3,2,1,0:T(8,128)(2,1)} reshape(bf16[512,2048]{1,0:T(8,128)(2,1)S(1)} %get-tuple-element.432) | data formatting | bytes 4194304 | tf_op jit(solution)/shard_map/while/body/eval_jaxpr/reshape | solution.py:89
  413.6 8.6 %copy.92 = bf16[64,8,64,32]{2,3,1,0:T(8,128)(2,1)} copy(bf16[64,8,64,32]{3,2,1,0:T(8,128)(2,1)} %reshape.221) | data formatting | bytes 4194304 | tf_op jit(solution)/shard_map/while/body/eval_jaxpr/reshape | solution.py:89
  422.2 2.9 gather_fusion
  431.5 8.0 %reshape.221 = bf16[64,8,64,32]{3,2,1,0:T(8,128)(2,1)} reshape(bf16[512,2048]{1,0:T(8,128)(2,1)S(1)} %get-tuple-element.432) | data formatting | bytes 4194304 | tf_op jit(solution)/shard_map/while/body/eval_jaxpr/reshape | solution.py:89
  439.6 8.6 %copy.92 = bf16[64,8,64,32]{2,3,1,0:T(8,128)(2,1)} copy(bf16[64,8,64,32]{3,2,1,0:T(8,128)(2,1)} %reshape.221) | data formatting | bytes 4194304 | tf_op jit(solution)/shard_map/while/body/eval_jaxpr/reshape | solution.py:89
  448.2 2.9 gather_fusion
  457.5 8.0 %reshape.221 = bf16[64,8,64,32]{3,2,1,0:T(8,128)(2,1)} reshape(bf16[512,2048]{1,0:T(8,128)(2,1)S(1)} %get-tuple-element.432) | data formatting | bytes 4194304 | tf_op jit(solution)/shard_map/while/body/eval_jaxpr/reshape | solution.py:89
  465.6 8.6 %copy.92 = bf16[64,8,64,32]{2,3,1,0:T(8,128)(2,1)} copy(bf16[64,8,64,32]{3,2,1,0:T(8,128)(2,1)} %reshape.221) | data formatting | bytes 4194304 | tf_op jit(solution)/shard_map/while/body/eval_jaxpr/reshape | solution.py:89
  474.1 2.9 gather_fusion
  (160 shorter events, 81.6 us)
Async XLA Ops:
  6.5 280.3 %all-reduce.3.cloned.1.call-start = ((), (), s32[]{:S(2)}) async-start(), calls=%async_computation | async-start | bytes 8650752 | tf_op jit(solution)/shard_map/psum | solution.py:156
  8.0 5.3 %copy-start.1 = (bf16[256,256]{1,0:T(8,128)(2,1)S(1)}, bf16[256,256]{1,0:T(8,128)(2,1)}, u32[]{:S(2)}) copy-start(bf16[256,256]{1,0:T(8,128)(2,1)} %get-tuple-element.403) | copy-start | bytes 393220 | tf_op jit(solution)/shard_map/while
  11.5 3.1 copy-start.5
  11.5 3.1 copy-start.6
  18.3 3.5 copy-start.2
  35.2 5.3 %copy-start.1 = (bf16[256,256]{1,0:T(8,128)(2,1)S(1)}, bf16[256,256]{1,0:T(8,128)(2,1)}, u32[]{:S(2)}) copy-start(bf16[256,256]{1,0:T(8,128)(2,1)} %get-tuple-element.403) | copy-start | bytes 393220 | tf_op jit(solution)/shard_map/while
  38.8 3.1 copy-start.5
  38.8 3.1 copy-start.6
  45.5 3.5 copy-start.2
  64.6 5.3 %copy-start.1 = (bf16[256,256]{1,0:T(8,128)(2,1)S(1)}, bf16[256,256]{1,0:T(8,128)(2,1)}, u32[]{:S(2)}) copy-start(bf16[256,256]{1,0:T(8,128)(2,1)} %get-tuple-element.403) | copy-start | bytes 393220 | tf_op jit(solution)/shard_map/while
  68.1 3.1 copy-start.5
  68.1 3.1 copy-start.6
  74.8 3.5 copy-start.2
  94.0 5.3 %copy-start.1 = (bf16[256,256]{1,0:T(8,128)(2,1)S(1)}, bf16[256,256]{1,0:T(8,128)(2,1)}, u32[]{:S(2)}) copy-start(bf16[256,256]{1,0:T(8,128)(2,1)} %get-tuple-element.403) | copy-start | bytes 393220 | tf_op jit(solution)/shard_map/while
  97.5 3.1 copy-start.5
  97.5 3.1 copy-start.6
  104.2 3.5 copy-start.2
  301.3 3.1 copy-start.3
  319.3 8.9 %copy-start = (bf16[512,64,32]{0,2,1:T(8,128)(2,1)S(1)}, bf16[512,64,32]{0,2,1:T(8,128)(2,1)}, u32[]{:S(2)}) copy-start(bf16[512,64,32]{0,2,1:T(8,128)(2,1)} %fusion.35) | copy-start | bytes 6291460
  369.4 9.9 %copy-start.4 = (bf16[256,256]{1,0:T(8,128)(2,1)S(1)}, bf16[256,256]{1,0:T(8,128)(2,1)}, u32[]{:S(2)}) copy-start(bf16[256,256]{1,0:T(8,128)(2,1)} %param.23) | copy-start | bytes 393220
Sparse Core Ops, SparseCore 0:
  129.3 157.4 all-reduce.2
where the time goes:
time: 493 us; the launch traced here: 490 us
  local copies, waits for them, and re-layouts  182 us (37%)
  waiting for transfers between devices  158 us (32%)
  matrix products  84 us (17%)
  other arithmetic  52.1 us (11%)
  between operations  13.5 us (3%)
    psum x1, waiting for transfers between devices, on_device(): lax.psum((domain_accumulated.reshape(MESHES * attention_group_amount, -1)...  158 us
    reshape x8, local copies, waits for them, and re-layouts, spread_phase(): tokens.reshape(MESHES, attention_group_amount, partition_amount, head_width)  66.4 us
    dot_general x4, matrix products, partition_routine(): jnp.dot(one_hot.T, partial_sums.reshape(tile_amount, -1))  17.9 us
    sub x4, matrix products, partition_routine(): jax.nn.softmax(partition_scores, axis=-1) * living[:, :, None, None]  14.4 us
    reshape x4, local copies, waits for them, and re-layouts, partition_routine(): partial_sums.reshape(tile_amount, -1)  14 us
    reduce_sum x4, other arithmetic, partition_routine(): partial_totals = jnp.sum(partition_shares.astype(jnp.float32), axis=1)  13.5 us
    dot_general x1, matrix products, attend_tokens(): jnp.einsum('rme,rne->rmn', queries, key_rows) * head_width ** (-0.5)  12.5 us
    gather x4, local copies, waits for them, and re-layouts, spread_phase(): chosen = jnp.take(tables, jnp.minimum(domain_sequence, MESHES - 1), axis=0)  11.7 us
  transfers between devices with their start and end apart: 1, of which 1 were waited for; matrix products, arithmetic and copies ran while one was open for 0% of the time, Pallas kernels for 0%

commit v1 on v0

--- a/solution.py
+++ b/solution.py
@@ -154,11 +154,14 @@
         gather_step, initial, grouped
     )
     whole_sums, whole_totals = lax.psum(
-        (
-            domain_accumulated.reshape(MESHES * attention_group_amount, -1),
-            domain_share_accumulated.reshape(MESHES * attention_group_amount, -1),
+        lax.psum(
+            (
+                domain_accumulated.reshape(MESHES * attention_group_amount, -1),
+                domain_share_accumulated.reshape(MESHES * attention_group_amount, -1),
+            ),
+            "grp",
         ),
-        ("grp", "dev"),
+        "dev",
     )
     tokens = attend_tokens(whole_sums, whole_totals, partition_attention_maps)
 

time: 493 us -> 681 us (1.38)
  waiting for transfers between devices: 158 us -> 345 us
    psum x0 -> x1, waiting for transfers between devices: none -> 155 us  [on_device(): lax.psum(lax.psum((domain_accumulated.reshape(MESHES * attention_group_am...]
    psum x1, waiting for transfers between devices: 158 us -> 191 us  [on_device(): lax.psum((domain_accumulated.reshape(MESHES * attention_group_amount, -1)...]
  transfers between devices with their start and end apart: 1 -> 2, of which waited for: 1 -> 2; matrix products, arithmetic and copies ran while one was open for 0% -> 0% of each run, Pallas kernels for 0% -> 0%
where the time goes in v1:
time: 681 us; the launch traced here: 678 us
  waiting for transfers between devices  345 us (51%)
  local copies, waits for them, and re-layouts  182 us (27%)
  matrix products  84 us (12%)
  other arithmetic  52.1 us (8%)
  between operations  13.5 us (2%)
    psum x1, waiting for transfers between devices, on_device(): lax.psum((domain_accumulated.reshape(MESHES * attention_group_amount, -1)...  191 us
    psum x1, waiting for transfers between devices, on_device(): lax.psum(lax.psum((domain_accumulated.reshape(MESHES * attention_group_am...  155 us
    reshape x8, local copies, waits for them, and re-layouts, spread_phase(): tokens.reshape(MESHES, attention_group_amount, partition_amount, head_width)  66.4 us
    dot_general x4, matrix products, partition_routine(): jnp.dot(one_hot.T, partial_sums.reshape(tile_amount, -1))  17.9 us
    sub x4, matrix products, partition_routine(): jax.nn.softmax(partition_scores, axis=-1) * living[:, :, None, None]  14.4 us
    reshape x4, local copies, waits for them, and re-layouts, partition_routine(): partial_sums.reshape(tile_amount, -1)  14 us
  transfers between devices with their start and end apart: 2, of which 2 were waited for; matrix products, arithmetic and copies ran while one was open for 0% of the time, Pallas kernels for 0%

profile of v1, /device:TPU:1, one launch (start us, length us, event | category | flops | bytes accessed | tf_op | source)
XLA Modules:
  0.0 678.0 jit_solution(13464356286495240531)
XLA Ops:
  8.0 115.3 %while.26 = (s32[]{:T(128)}, f32[64,16384]{1,0:T(8,128)}, f32[64,512]{1,0:T(8,128)S(1)}, bf16[4,16,128,512]{2,3,1,0:T(8,128)(2,1)}, s32[4,16]{1,0:T(4,128)S(1)},...) while((s32[]{:T(128)}, f32[64,16384]{1,0:T(8,128)}, ...), condition=%wide.region_6.7_spmd.clone, body=%wide.region_0.6_spmd.clone.sunk | while | flops 723058752 | bytes 48028012 | solution.py:153
  14.7 3.6 fusion.111
  18.4 3.4 convert_reduce_fusion.5
  24.9 2.1 fusion.112
  27.0 3.5 reshape.222
  30.5 2.8 convolution_add_fusion.5
  41.9 3.6 fusion.111
  45.6 3.4 convert_reduce_fusion.5
  54.2 3.5 reshape.222
  57.7 5.0 convolution_add_fusion.5
  71.3 3.6 fusion.111
  74.9 3.4 convert_reduce_fusion.5
  83.5 3.5 reshape.222
  87.0 5.0 convolution_add_fusion.5
  100.6 3.6 fusion.111
  104.3 3.4 convert_reduce_fusion.5
  112.9 3.5 reshape.222
  116.4 5.0 convolution_add_fusion.5
  123.3 4.9 reshape.192
  129.4 190.6 %all-reduce.7.cloned.1.call-done = (f32[512,2048]{1,0:T(8,128)}, f32[512,64]{0,1:T(8,128)}) async-done(((f32[512,2048]{1,0:T(8,128)}, f32[512,64]{0,1:T(8,128)}), (f32[512,2048]{1,0:T(8,128)}, f32[512,64]{0,1:T(8,128)})) %all-reduce.7.cloned.1.call-update) | async-done | bytes 4325392 | tf_op jit(solution)/shard_map/psum | solution.py:157
  320.1 154.7 %all-reduce.5.cloned.1.call-done = (f32[512,2048]{1,0:T(8,128)}, f32[512,64]{0,1:T(8,128)}) async-done(((f32[512,2048]{1,0:T(8,128)}, f32[512,64]{0,1:T(8,128)}), (f32[512,2048]{1,0:T(8,128)}, f32[512,64]{0,1:T(8,128)})) %all-reduce.5.cloned.1.call-update) | async-done | bytes 4325392 | tf_op jit(solution)/shard_map/psum | solution.py:156
  475.7 2.5 div.47
  478.2 5.4 copy.52
  483.6 5.7 div.49
  489.2 2.9 copy.53
  492.1 2.1 fusion.39
  496.2 2.1 fusion.35
  498.3 8.8 %copy.56 = bf16[512,64,32]{1,2,0:T(8,128)(2,1)} copy(bf16[512,64,32]{0,2,1:T(8,128)(2,1)} %fusion.39) | data formatting | bytes 4194304 | tf_op jit(solution)/shard_map/rmd,de->rme/dot_general | solution.py:73
  507.1 8.9 %copy.57 = bf16[512,64,32]{1,2,0:T(8,128)(2,1)} copy(bf16[512,64,32]{0,2,1:T(8,128)(2,1)} %fusion.37) | data formatting | bytes 4194304 | tf_op jit(solution)/shard_map/rmd,de->rme/dot_general | solution.py:74
  516.0 7.9 %copy.60 = bf16[512,64,32]{1,2,0:T(8,128)(2,1)} copy(bf16[512,64,32]{0,2,1:T(8,128)(2,1)S(1)} %copy-done) | data formatting | bytes 4194304 | tf_op jit(solution)/shard_map/rmd,de->rme/dot_general | solution.py:75
  523.9 12.5 %multiply_reduce_fusion.1 = (f32[512,64]{1,0:T(8,128)S(1)}, f32[512,64,64]{1,2,0:T(8,128)}) fusion(bf16[512,64,32]{1,2,0:T(8,128)(2,1)} %copy.56, bf16[512,64,32]{1,2,0:T(8,128)(2,1)} %copy.57), kind=kOutput, calls=%fused_computation.61 | convolution fusion | flops 138379264 | bytes 12713984 | tf_op jit(solution)/shard_map/rme,rne->rmn/dot_general | solution.py:76
  536.4 10.3 %fusion.28 = f32[512,64]{1,0:T(8,128)S(1)} fusion(f32[512,64,64]{1,2,0:T(8,128)} %get-tuple-element.231, f32[512,64]{1,0:T(8,128)S(1)} %get-tuple-element.230), kind=kLoop, calls=%fused_computation.62 | loop fusion | flops 6258688 | bytes 8650752 | tf_op jit(solution)/shard_map/reduce_sum | solution.py:77
  546.7 10.4 %fusion.32 = bf16[512,64,32]{1,2,0:T(8,128)(2,1)} fusion(bf16[512,64,32]{1,2,0:T(8,128)(2,1)} %copy.60, f32[512,64,64]{1,2,0:T(8,128)} %get-tuple-element.231, f32[512,64]{1,0:T(8,128)S(1)} %fusion.28, f32[512,64]{1,0:T(8,128)S(1)} %get-tuple-element.230), kind=kOutput, calls=%fused_computation.66 | convolution fusion | flops 140509184 | bytes 12845056 | tf_op jit(solution)/shard_map/rmn,rne->rme/dot_general | solution.py:78
  557.1 6.9 %copy.61 = bf16[512,64,32]{0,2,1:T(8,128)(2,1)} copy(bf16[512,64,32]{1,2,0:T(8,128)(2,1)} %fusion.32) | data formatting | bytes 4194304 | tf_op jit(solution)/shard_map/convert_element_type | solution.py:79
  564.0 2.9 copy.62
  567.0 104.2 %while.25 = (s32[]{:T(128)}, bf16[4,16,128,256]{3,2,1,0:T(8,128)(2,1)}, bf16[4,16,128,256]{3,2,1,0:T(8,128)(2,1)}, s32[4,16]{1,0:T(4,128)S(1)}, bf16[512,2048]{1...) while((s32[]{:T(128)}, ...), condition=%wide.region_14.15_spmd, body=%wide.region_13.14_spmd.sunk | while | flops 338433216 | bytes 26891408 | solution.py:178
  567.3 8.0 %reshape.221 = bf16[64,8,64,32]{3,2,1,0:T(8,128)(2,1)} reshape(bf16[512,2048]{1,0:T(8,128)(2,1)S(1)} %get-tuple-element.434) | data formatting | bytes 4194304 | tf_op jit(solution)/shard_map/while/body/eval_jaxpr/reshape | solution.py:89
  575.3 8.6 %copy.92 = bf16[64,8,64,32]{2,3,1,0:T(8,128)(2,1)} copy(bf16[64,8,64,32]{3,2,1,0:T(8,128)(2,1)} %reshape.221) | data formatting | bytes 4194304 | tf_op jit(solution)/shard_map/while/body/eval_jaxpr/reshape | solution.py:89
  583.9 2.9 gather_fusion
  593.3 8.0 %reshape.221 = bf16[64,8,64,32]{3,2,1,0:T(8,128)(2,1)} reshape(bf16[512,2048]{1,0:T(8,128)(2,1)S(1)} %get-tuple-element.434) | data formatting | bytes 4194304 | tf_op jit(solution)/shard_map/while/body/eval_jaxpr/reshape | solution.py:89
  601.3 8.6 %copy.92 = bf16[64,8,64,32]{2,3,1,0:T(8,128)(2,1)} copy(bf16[64,8,64,32]{3,2,1,0:T(8,128)(2,1)} %reshape.221) | data formatting | bytes 4194304 | tf_op jit(solution)/shard_map/while/body/eval_jaxpr/reshape | solution.py:89
  609.9 2.9 gather_fusion
  619.3 8.0 %reshape.221 = bf16[64,8,64,32]{3,2,1,0:T(8,128)(2,1)} reshape(bf16[512,2048]{1,0:T(8,128)(2,1)S(1)} %get-tuple-element.434) | data formatting | bytes 4194304 | tf_op jit(solution)/shard_map/while/body/eval_jaxpr/reshape | solution.py:89
  627.3 8.6 %copy.92 = bf16[64,8,64,32]{2,3,1,0:T(8,128)(2,1)} copy(bf16[64,8,64,32]{3,2,1,0:T(8,128)(2,1)} %reshape.221) | data formatting | bytes 4194304 | tf_op jit(solution)/shard_map/while/body/eval_jaxpr/reshape | solution.py:89
  635.9 2.9 gather_fusion
  645.2 8.0 %reshape.221 = bf16[64,8,64,32]{3,2,1,0:T(8,128)(2,1)} reshape(bf16[512,2048]{1,0:T(8,128)(2,1)S(1)} %get-tuple-element.434) | data formatting | bytes 4194304 | tf_op jit(solution)/shard_map/while/body/eval_jaxpr/reshape | solution.py:89
  653.3 8.6 %copy.92 = bf16[64,8,64,32]{2,3,1,0:T(8,128)(2,1)} copy(bf16[64,8,64,32]{3,2,1,0:T(8,128)(2,1)} %reshape.221) | data formatting | bytes 4194304 | tf_op jit(solution)/shard_map/while/body/eval_jaxpr/reshape | solution.py:89
  661.8 2.9 gather_fusion
  (163 shorter events, 83.9 us)
Async XLA Ops:
  6.5 313.5 %all-reduce.7.cloned.1.call-start = ((), (), s32[]{:S(2)}) async-start(), calls=%async_computation.1 | async-start | bytes 8650752 | tf_op jit(solution)/shard_map/psum | solution.py:157
  8.0 5.3 copy-start.1
  11.5 3.1 copy-start.5
  11.5 3.1 copy-start.6
  18.3 3.5 copy-start.2
  35.2 5.3 copy-start.1
  38.8 3.1 copy-start.5
  38.8 3.1 copy-start.6
  45.5 3.5 copy-start.2
  64.6 5.3 copy-start.1
  68.1 3.1 copy-start.5
  68.1 3.1 copy-start.6
  74.8 3.5 copy-start.2
  93.9 5.3 copy-start.1
  97.5 3.1 copy-start.5
  97.5 3.1 copy-start.6
  104.2 3.5 copy-start.2
  129.2 345.6 %all-reduce.5.cloned.1.call-start = ((), (), s32[]{:S(2)}) async-start(), calls=%async_computation | async-start | bytes 8650752 | tf_op jit(solution)/shard_map/psum | solution.py:156
  489.2 2.9 copy-start.3
  507.1 8.9 %copy-start = (bf16[512,64,32]{0,2,1:T(8,128)(2,1)S(1)}, bf16[512,64,32]{0,2,1:T(8,128)(2,1)}, u32[]{:S(2)}) copy-start(bf16[512,64,32]{0,2,1:T(8,128)(2,1)} %fusion.35) | copy-start | bytes 6291460
  557.1 9.9 %copy-start.4 = (bf16[256,256]{1,0:T(8,128)(2,1)S(1)}, bf16[256,256]{1,0:T(8,128)(2,1)}, u32[]{:S(2)}) copy-start(bf16[256,256]{1,0:T(8,128)(2,1)} %param.23) | copy-start | bytes 393220
Sparse Core Ops, SparseCore 0:
  129.3 190.6 all-reduce.6
  322.6 152.0 all-reduce.4
